TPU v7x, 32 devices: a whole 2x2x4 slice. The times are simulated.
32 devices in a mesh: group: 8 (over z, x), rad: 4 (over y, core).
Axes of the slice: x: 2, y: 2, z: 4, core: 2. Of those that a mesh axis runs over, the one named last changes fastest.
Arguments:
- source_term: float32 [32, 128, 1024], P('group', 'rad'), may hold values from -6 to 6
- initial_guess: float32 [32, 128, 1024], P('group', 'rad'), may hold values from -3 to 3
- metric: float32 [3, 8, 32, 256], P(None, 'group', 'rad'), may hold values from 0.5 to 4
Outputs:
- solution: float32 [32, 128, 1024], P('group', 'rad')
- residual: float32 [32, 128, 1024], P('group', 'rad')
All inputs are finite; a program needn't handle non-finite values.
Results may differ from a plain program's by a relative error of at most 0.00025.
Values sent between devices are 32-bit elements; how exact they have to be, the bound alone decides.
A program may use at most 128 MiB of HBM per device.

v0:
```python
import math

import jax
import jax.numpy as jnp
import numpy as np
from jax import lax
from jax.sharding import PartitionSpec as P

ITERS = 3


def passed_along(block, axis, distance):
    devices = range(lax.axis_size(axis))
    route = [(i - distance, i) for i in devices if i - distance in devices]
    return lax.ppermute(block, axis, route)


def passed_along_2(value, axis, steps):
    count = lax.axis_size(axis)
    pairs = [(source, (source + steps) % count) for source in range(count)]
    return lax.ppermute(value, axis, pairs)


def gll_tables():
    root = math.sqrt(3.0 / 7.0)
    points = np.array([-1.0, -root, 0.0, root, 1.0])
    weights = np.array([0.1, 49.0 / 90.0, 32.0 / 45.0, 49.0 / 90.0, 0.1])
    factor = np.array(
        [np.prod([points[a] - points[m] for m in range(5) if m != a]) for a in range(5)]
    )
    derivative = np.zeros((5, 5))
    for p in range(5):
        for a in range(5):
            if p == a:
                derivative[p, a] = np.sum(
                    [1.0 / (points[a] - points[m]) for m in range(5) if m != a]
                )
            else:
                derivative[p, a] = factor[p] / (factor[a] * (points[p] - points[a]))
    return (jnp.asarray(derivative, jnp.float32), jnp.asarray(weights, jnp.float32))


def apply_elements(elements, metric):
    derivative, weights = gll_tables()
    quad_weight = (
        weights[:, None, None] * weights[None, :, None] * weights[None, None, :]
    ).reshape(5, 5, 5, 1, 1, 1)
    high = lax.Precision.HIGHEST
    grad_x = jnp.einsum("pa,abcxyz->pbcxyz", derivative, elements, precision=high)
    result_sum = jnp.einsum(
        "pa,pbcxyz->abcxyz", derivative, grad_x * quad_weight * metric[0], precision=high
    )
    grad_r = jnp.einsum("qb,abcxyz->aqcxyz", derivative, elements, precision=high)
    result_sum = result_sum + jnp.einsum(
        "qb,aqcxyz->abcxyz", derivative, grad_r * quad_weight * metric[1], precision=high
    )
    grad_y = jnp.einsum("sc,abcxyz->absxyz", derivative, elements, precision=high)
    result_sum = result_sum + jnp.einsum(
        "sc,absxyz->abcxyz", derivative, grad_y * quad_weight * metric[2], precision=high
    )
    return result_sum


def element_diagonal(metric):
    derivative, weights = gll_tables()
    squared = jnp.sum(derivative * derivative * weights[:, None], axis=0)
    term_x = (squared[:, None, None] * weights[None, :, None] * weights[None, None, :]).reshape(
        5, 5, 5, 1, 1, 1
    )
    term_r = (weights[:, None, None] * squared[None, :, None] * weights[None, None, :]).reshape(
        5, 5, 5, 1, 1, 1
    )
    term_y = (weights[:, None, None] * weights[None, :, None] * squared[None, None, :]).reshape(
        5, 5, 5, 1, 1, 1
    )
    return term_x * metric[0] + term_r * metric[1] + term_y * metric[2]


def to_blocks(field):
    rows_x, rows_r, rows_y = field.shape
    shaped = field.reshape(rows_x // 4, 4, rows_r // 4, 4, rows_y // 4, 4)
    return shaped.transpose(1, 3, 5, 0, 2, 4)


def from_blocks(blocks):
    count_x, count_r, count_y = (blocks.shape[3], blocks.shape[4], blocks.shape[5])
    return blocks.transpose(3, 0, 4, 1, 5, 2).reshape(4 * count_x, 4 * count_r, 4 * count_y)


def extend_y(wide):
    return jnp.concatenate([wide, jnp.roll(wide[:, :, 0:1], -1, axis=5)], 2)


def fold_y(raw):
    first = raw[:, :, 0:1] + jnp.roll(raw[:, :, 4:5], 1, axis=5)
    return jnp.concatenate([first, raw[:, :, 1:4]], 2)


def assemble(raw):
    folded = fold_y(raw)
    count_r = folded.shape[4]
    below_r = passed_along(folded[:, 4:5, :, :, count_r - 1 :], "rad", 1)
    carried = jnp.concatenate([below_r, folded[:, 4:5, :, :, : count_r - 1]], 4)
    folded = jnp.concatenate([folded[:, 0:1] + carried, folded[:, 1:4]], 1)
    count_x = folded.shape[3]
    below_x = passed_along_2(folded[4:5, :, :, count_x - 1 :], "group", 1)
    carried = jnp.concatenate([below_x, folded[4:5, :, :, : count_x - 1]], 3)
    return jnp.concatenate([folded[0:1] + carried, folded[1:4]], 0)


def paired_sums(residual, smoothed, applied):
    return lax.psum((jnp.sum(residual * smoothed), jnp.sum(applied * smoothed)), ("group", "rad"))


def local(source_term, initial_guess, metric):

    def operate(field):
        above_x = passed_along_2(field[0:1, :, :, 0:1], "group", -1)
        plane_a = jnp.concatenate([field[0:1, :, :, 1:], above_x], 3)
        wide = jnp.concatenate([field, plane_a], 0)
        above_r = passed_along(wide[:, 0:1, :, :, 0:1], "rad", -1)
        plane_b = jnp.concatenate([wide[:, 0:1, :, :, 1:], above_r], 4)
        wide = jnp.concatenate([wide, plane_b], 1)
        return assemble(apply_elements(extend_y(wide), metric))

    diagonal = assemble(element_diagonal(metric))
    scaling = 1.0 / diagonal
    guess = to_blocks(initial_guess)
    residual = to_blocks(source_term) - operate(guess)
    solution = guess
    smoothed = scaling * residual
    applied = operate(smoothed)
    weighted_norm, curvature_sum = paired_sums(residual, smoothed, applied)
    step_size = weighted_norm / curvature_sum
    direction = smoothed
    searched = applied
    for iteration in range(ITERS):
        solution = solution + step_size * direction
        residual = residual - step_size * searched
        if iteration + 1 < ITERS:
            smoothed = scaling * residual
            applied = operate(smoothed)
            next_norm, curvature_sum = paired_sums(residual, smoothed, applied)
            ratio = next_norm / weighted_norm
            step_size = next_norm / (curvature_sum - ratio * next_norm / step_size)
            direction = smoothed + ratio * direction
            searched = applied + ratio * searched
            weighted_norm = next_norm
    return (from_blocks(solution), from_blocks(residual))


def solution(mesh):
    in_specs = (P("group", "rad", None), P("group", "rad", None), P(None, "group", "rad", None))
    out_specs = (P("group", "rad", None), P("group", "rad", None))
    return jax.shard_map(local, mesh=mesh, in_specs=in_specs, out_specs=out_specs, check_vma=False)
```

profile of v0, /device:TPU:0, one launch (start us, length us, event | category | flops | bytes accessed | tf_op | source)
XLA Modules:
  0.0 408.9 jit_solution(13129689504433719481)
XLA Ops:
  0.6 19.5 %reshape.564 = f32[1,4,8,4,256,4]{5,4,3,2,1,0:T(8,128)} reshape(f32[4,32,1024]{2,1,0:T(8,128)} %param.14) | data formatting | bytes 1048576 | tf_op jit(solution)/shard_map/reshape | solution.py:81
  20.1 10.1 %copy.48 = f32[1,4,8,4,256,4]{4,1,2,5,3,0:T(4,128)S(1)} copy(f32[1,4,8,4,256,4]{5,4,3,2,1,0:T(8,128)} %reshape.564) | data formatting | bytes 1048576 | tf_op jit(solution)/shard_map/reshape | solution.py:81
  30.3 6.1 %collective-permute-start = (f32[1,4,4,1,8,256]{5,0,4,2,1,3:T(1,128)S(1)}, f32[1,4,4,1,8,256]{5,0,4,2,1,3:T(1,128)S(1)}, u32[]{:S(2)}, u32[]{:S(2)}) collective-permute-start(f32[1,4,4,1,8,256]{5,0,4,2,1,3:T(1,128)S(1)} %slice.355), channel_id=1, source_target_pairs={{0,28},{4,0},{8,4},{12,8},{16,12},{20,16},{24,20},{28,24},{1,29},{... | collective-permute-start | bytes 393224 | tf_op jit(solution)/shard_map/ppermute | solution.py:21
  36.6 18.6 %reshape.565 = f32[1,4,8,4,256,4]{5,4,3,2,1,0:T(8,128)} reshape(f32[4,32,1024]{2,1,0:T(8,128)S(1)} %copy-done.7) | data formatting | bytes 1048576 | tf_op jit(solution)/shard_map/reshape | solution.py:81
  55.3 10.0 %copy.49 = f32[1,4,8,4,256,4]{4,1,2,5,3,0:T(4,128)S(1)} copy(f32[1,4,8,4,256,4]{5,4,3,2,1,0:T(8,128)} %reshape.565) | data formatting | bytes 1048576 | tf_op jit(solution)/shard_map/reshape | solution.py:81
  68.9 2.2 fusion.62
  71.2 2.2 fusion.66
  73.4 1.8 fusion.122
  76.3 2.1 fusion.64
  80.1 14.8 %bitcast_add_fusion.6 = f32[5,5,5,1,8,256]{5,0,4,2,1,3:T(8,128)S(1)} fusion(f32[5,5,8,256,5]{3,4,2,1,0:T(8,128)S(1)} %fusion.32, f32[5,5,8,256,5]{3,4,2,1,0:T(8,128)S(1)} %fusion.64, f32[5,5,1,1,1]{0,1,4,3,2:T(8,128)S(1)} %copy-done.4, f32[5,5,5,8,256]{4,0,3,2,1:T(8,128)S(1)} %fusion.122, f32[8,256]{1,0:T(8,128)S(1)} %get-tuple-element.21, ...), kind=kOutput, calls=%fused_computation.57 | convolution fusion | flops 16384000 | bytes 4104792 | tf_op jit(solution)/shard_map/pa,pbcxyz->abcxyz/dot_general | solution.py:50
  95.5 3.9 collective-permute-start.2
  99.6 1.9 collective-permute-start.4
  102.9 8.2 %collective-permute-done.3 = f32[1,4,4,1,8,256]{5,0,4,2,1,3:T(1,128)S(1)} collective-permute-done((f32[1,4,4,1,8,256]{5,0,4,2,1,3:T(1,128)S(1)}, f32[1,4,4,1,8,256]{5,0,4,2,1,3:T(1,128)S(1)}, u32[]{:S(2)}, u32[]{:S(2)}) %collective-permute-start.3) | collective-permute-done | bytes 131104 | tf_op jit(solution)/shard_map/ppermute | solution.py:21
  113.9 5.0 %collective-permute-done.6 = f32[1,4,4,1,8,256]{5,0,4,2,1,3:T(1,128)S(1)} collective-permute-done((f32[1,4,4,1,8,256]{5,0,4,2,1,3:T(1,128)S(1)}, f32[1,4,4,1,8,256]{5,0,4,2,1,3:T(1,128)S(1)}, u32[]{:S(2)}, u32[]{:S(2)}) %collective-permute-start.6) | collective-permute-done | bytes 131104 | tf_op jit(solution)/shard_map/ppermute | solution.py:21
  122.4 2.2 fusion.56
  124.6 2.1 fusion.60
  126.8 1.8 fusion.123
  130.9 2.1 fusion.58
  133.0 3.0 bitcast_add_fusion.4
  136.5 2.4 collective-permute-start.8
  140.2 8.3 %collective-permute-done.9 = f32[1,4,4,1,8,256]{5,0,4,2,1,3:T(1,128)S(1)} collective-permute-done((f32[1,4,4,1,8,256]{5,0,4,2,1,3:T(1,128)S(1)}, f32[1,4,4,1,8,256]{5,0,4,2,1,3:T(1,128)S(1)}, u32[]{:S(2)}, u32[]{:S(2)}) %collective-permute-start.9) | collective-permute-done | bytes 131104 | tf_op jit(solution)/shard_map/ppermute | solution.py:21
  149.8 37.1 %all-reduce.2 = (f32[]{:T(128)}, f32[]{:T(128)}) all-reduce(f32[]{:T(128)} %get-tuple-element.7, f32[]{:T(128)} %get-tuple-element.6), channel_id=1, replica_groups=mesh['group'=8,'rad'=4] {'group','rad'}, use_global_device_ids=true, to_apply=%region_2.3 | all-reduce | flops 2 | bytes 16 | tf_op jit(solution)/shard_map/psum | solution.py:112
  189.9 4.0 collective-permute-start.10
  194.0 2.5 collective-permute-done.10
  200.1 2.2 fusion.50
  202.3 2.1 fusion.54
  204.4 1.8 fusion.124
  208.5 2.1 fusion.52
  210.7 2.8 bitcast_add_fusion.2
  213.9 4.2 %collective-permute-start.12 = (f32[5,1,4,1,1,256]{5,0,4,2,1,3:T(8,128)S(1)}, f32[5,1,4,1,1,256]{5,0,4,2,1,3:T(8,128)S(1)}, u32[]{:S(2)}, u32[]{:S(2)}) collective-permute-start(f32[5,1,4,1,1,256]{5,0,4,2,1,3:T(8,128)S(1)} %pad_maximum_fusion.30), channel_id=1, source_target_pairs={{0,1},{1,2},{2,3},{4,5},{5,6},{6,7},{8,9},{9,10},{10,11},{12,13},{... | collective-permute-start | bytes 61448 | tf_op jit(solution)/shard_map/ppermute | solution.py:15
  221.1 7.4 %collective-permute-done.13 = f32[1,4,4,1,8,256]{5,0,4,2,1,3:T(1,128)S(1)} collective-permute-done((f32[1,4,4,1,8,256]{5,0,4,2,1,3:T(1,128)S(1)}, f32[1,4,4,1,8,256]{5,0,4,2,1,3:T(1,128)S(1)}, u32[]{:S(2)}, u32[]{:S(2)}) %collective-permute-start.13) | collective-permute-done | bytes 131104 | tf_op jit(solution)/shard_map/ppermute | solution.py:21
  230.5 38.6 %all-reduce.1 = (f32[]{:T(128)}, f32[]{:T(128)}) all-reduce(f32[]{:T(128)} %get-tuple-element.5, f32[]{:T(128)} %get-tuple-element.4), channel_id=1, replica_groups=mesh['group'=8,'rad'=4] {'group','rad'}, use_global_device_ids=true, to_apply=%region_6.7 | all-reduce | flops 2 | bytes 16 | tf_op jit(solution)/shard_map/psum | solution.py:112
  273.4 2.0 fusion.119
  275.6 3.3 collective-permute-start.14
  278.9 2.5 collective-permute-done.14
  285.0 2.2 fusion.44
  287.2 2.1 fusion.48
  289.3 1.8 fusion.125
  293.4 2.1 fusion.46
  295.6 2.9 bitcast_add_fusion
  298.8 4.1 %collective-permute-start.16 = (f32[5,1,4,1,1,256]{5,0,4,2,1,3:T(8,128)S(1)}, f32[5,1,4,1,1,256]{5,0,4,2,1,3:T(8,128)S(1)}, u32[]{:S(2)}, u32[]{:S(2)}) collective-permute-start(f32[5,1,4,1,1,256]{5,0,4,2,1,3:T(8,128)S(1)} %pad_maximum_fusion.28), channel_id=1, source_target_pairs={{0,1},{1,2},{2,3},{4,5},{5,6},{6,7},{8,9},{9,10},{10,11},{12,13},{... | collective-permute-start | bytes 61448 | tf_op jit(solution)/shard_map/ppermute | solution.py:15
  305.7 7.0 %collective-permute-done.17 = f32[1,4,4,1,8,256]{5,0,4,2,1,3:T(1,128)S(1)} collective-permute-done((f32[1,4,4,1,8,256]{5,0,4,2,1,3:T(1,128)S(1)}, f32[1,4,4,1,8,256]{5,0,4,2,1,3:T(1,128)S(1)}, u32[]{:S(2)}, u32[]{:S(2)}) %collective-permute-start.17) | collective-permute-done | bytes 131104 | tf_op jit(solution)/shard_map/ppermute | solution.py:21
  314.1 38.3 %all-reduce = (f32[]{:T(128)}, f32[]{:T(128)}) all-reduce(f32[]{:T(128)} %get-tuple-element.3, f32[]{:T(128)} %get-tuple-element.2), channel_id=1, replica_groups=mesh['group'=8,'rad'=4] {'group','rad'}, use_global_device_ids=true, to_apply=%region_10.11 | all-reduce | flops 2 | bytes 16 | tf_op jit(solution)/shard_map/psum | solution.py:112
  356.1 2.9 subtract_bitcast_fusion
  359.0 9.6 %copy.84 = f32[1,4,8,4,256,4]{5,4,3,2,1,0:T(8,128)} copy(f32[1,4,8,4,256,4]{4,1,2,5,3,0:T(4,128)} %get-tuple-element.32) | data formatting | bytes 1048576 | tf_op jit(solution)/shard_map/transpose | solution.py:87
  368.6 15.8 %reshape.579 = f32[4,32,1024]{2,1,0:T(8,128)} reshape(f32[1,4,8,4,256,4]{5,4,3,2,1,0:T(8,128)} %copy.84) | data formatting | bytes 1048576 | tf_op jit(solution)/shard_map/reshape | solution.py:87
  384.4 8.5 %copy.83 = f32[1,4,8,4,256,4]{5,4,3,2,1,0:T(8,128)} copy(f32[1,4,8,4,256,4]{4,1,2,5,3,0:T(4,128)S(1)} %copy-done.5) | data formatting | bytes 1048576 | tf_op jit(solution)/shard_map/transpose | solution.py:87
  392.9 15.7 %reshape.578 = f32[4,32,1024]{2,1,0:T(8,128)} reshape(f32[1,4,8,4,256,4]{5,4,3,2,1,0:T(8,128)} %copy.83) | data formatting | bytes 1048576 | tf_op jit(solution)/shard_map/reshape | solution.py:87
  (126 shorter events, 43.5 us)
Async XLA Ops:
  20.1 16.3 %copy-start.9 = (f32[5]{0:T(128)S(1)}, f32[5]{0:T(128)}, u32[]{:S(2)}) copy-start(f32[5]{0:T(128)} %constant.15) | copy-start | bytes 64
  20.1 16.3 %copy-start.10 = (f32[5]{0:T(128)S(1)}, f32[5]{0:T(128)}, u32[]{:S(2)}) copy-start(f32[5]{0:T(128)} %constant.9.clone) | copy-start | bytes 64
  20.1 16.5 %copy-start.7 = (f32[4,32,1024]{2,1,0:T(8,128)S(1)}, f32[4,32,1024]{2,1,0:T(8,128)}, u32[]{:S(2)}) copy-start(f32[4,32,1024]{2,1,0:T(8,128)} %param.13) | copy-start | bytes 1572868
  30.3 35.0 %collective-permute-start = (f32[1,4,4,1,8,256]{5,0,4,2,1,3:T(1,128)S(1)}, f32[1,4,4,1,8,256]{5,0,4,2,1,3:T(1,128)S(1)}, u32[]{:S(2)}, u32[]{:S(2)}) collective-permute-start(f32[1,4,4,1,8,256]{5,0,4,2,1,3:T(1,128)S(1)} %slice.355), channel_id=1, source_target_pairs={{0,28},{4,0},{8,4},{12,8},{16,12},{20,16},{24,20},{28,24},{1,29},{... | collective-permute-start | bytes 393224 | tf_op jit(solution)/shard_map/ppermute | solution.py:21
  55.3 10.0 %copy-start.8 = (f32[3,1,8,256]{3,2,1,0:T(8,128)S(1)}, f32[3,1,8,256]{3,2,1,0:T(8,128)}, u32[]{:S(2)}) copy-start(f32[3,1,8,256]{3,2,1,0:T(8,128)} %param.15) | copy-start | bytes 73732
  65.4 3.6 copy-start.4
  65.4 3.1 collective-permute-start.1
  95.5 6.1 %collective-permute-start.2 = (f32[5,1,4,1,1,256]{5,0,4,2,1,3:T(8,128)S(1)}, f32[5,1,4,1,1,256]{5,0,4,2,1,3:T(8,128)S(1)}, u32[]{:S(2)}, u32[]{:S(2)}) collective-permute-start(f32[5,1,4,1,1,256]{5,0,4,2,1,3:T(8,128)S(1)} %pad_maximum_fusion.35), channel_id=1, source_target_pairs={{0,1},{1,2},{2,3},{4,5},{5,6},{6,7},{8,9},{9,10},{10,11},{12,13},{... | collective-permute-start | bytes 61448 | tf_op jit(solution)/shard_map/ppermute | solution.py:15
  99.6 2.8 collective-permute-start.4
  102.0 9.1 %collective-permute-start.3 = (f32[1,4,4,1,8,256]{5,0,4,2,1,3:T(1,128)S(1)}, f32[1,4,4,1,8,256]{5,0,4,2,1,3:T(1,128)S(1)}, u32[]{:S(2)}, u32[]{:S(2)}) collective-permute-start(f32[1,4,4,1,8,256]{5,0,4,2,1,3:T(1,128)S(1)} %slice.361), channel_id=1, source_target_pairs={{0,4},{4,8},{8,12},{12,16},{16,20},{20,24},{24,28},{28,0},{1,5},{5... | collective-permute-start | bytes 393224 | tf_op jit(solution)/shard_map/ppermute | solution.py:21
  102.8 85.4 %copy-start = (f32[3,4,4,1,8,256]{5,0,4,2,1,3:T(4,128)}, f32[3,4,4,1,8,256]{5,0,4,2,1,3:T(4,128)S(1)}, u32[]{:S(2)}) copy-start(f32[3,4,4,1,8,256]{5,0,4,2,1,3:T(4,128)S(1)} %slice.369) | copy-start | bytes 1179652
  102.8 10.1 %collective-permute-start.5 = (f32[1,4,4,1,8,256]{5,0,4,2,1,3:T(1,128)S(1)}, f32[1,4,4,1,8,256]{5,0,4,2,1,3:T(1,128)S(1)}, u32[]{:S(2)}, u32[]{:S(2)}) collective-permute-start(f32[1,4,4,1,8,256]{5,0,4,2,1,3:T(1,128)S(1)} %slice.368), channel_id=1, source_target_pairs={{0,4},{4,8},{8,12},{12,16},{16,20},{20,24},{24,28},{28,0},{1,5},{5... | collective-permute-start | bytes 393224 | tf_op jit(solution)/shard_map/ppermute | solution.py:21
  113.7 34.9 %copy-start.3 = (f32[4,4,4,1,8,256]{5,0,4,2,1,3:T(4,128)}, f32[4,4,4,1,8,256]{5,0,4,2,1,3:T(4,128)S(1)}, u32[]{:S(2)}) copy-start(f32[4,4,4,1,8,256]{5,0,4,2,1,3:T(4,128)S(1)} %get-tuple-element.19) | copy-start | bytes 1572868
  113.8 5.0 %collective-permute-start.6 = (f32[1,4,4,1,8,256]{5,0,4,2,1,3:T(1,128)S(1)}, f32[1,4,4,1,8,256]{5,0,4,2,1,3:T(1,128)S(1)}, u32[]{:S(2)}, u32[]{:S(2)}) collective-permute-start(f32[1,4,4,1,8,256]{5,0,4,2,1,3:T(1,128)S(1)} %slice.370), channel_id=1, source_target_pairs={{0,28},{4,0},{8,4},{12,8},{16,12},{20,16},{24,20},{28,24},{1,29},{... | collective-permute-start | bytes 393224 | tf_op jit(solution)/shard_map/ppermute | solution.py:21
  118.9 3.1 collective-permute-start.7
  136.5 3.2 collective-permute-start.8
  140.0 8.5 %collective-permute-start.9 = (f32[1,4,4,1,8,256]{5,0,4,2,1,3:T(1,128)S(1)}, f32[1,4,4,1,8,256]{5,0,4,2,1,3:T(1,128)S(1)}, u32[]{:S(2)}, u32[]{:S(2)}) collective-permute-start(f32[1,4,4,1,8,256]{5,0,4,2,1,3:T(1,128)S(1)} %slice.376), channel_id=1, source_target_pairs={{0,4},{4,8},{8,12},{12,16},{16,20},{20,24},{24,28},{28,0},{1,5},{5... | collective-permute-start | bytes 393224 | tf_op jit(solution)/shard_map/ppermute | solution.py:21
  189.9 6.6 %collective-permute-start.10 = (f32[1,4,4,1,8,256]{5,0,4,2,1,3:T(1,128)S(1)}, f32[1,4,4,1,8,256]{5,0,4,2,1,3:T(1,128)S(1)}, u32[]{:S(2)}, u32[]{:S(2)}) collective-permute-start(f32[1,4,4,1,8,256]{5,0,4,2,1,3:T(1,128)S(1)} %slice.378), channel_id=1, source_target_pairs={{0,28},{4,0},{8,4},{12,8},{16,12},{20,16},{24,20},{28,24},{1,29},{... | collective-permute-start | bytes 393224 | tf_op jit(solution)/shard_map/ppermute | solution.py:21
  196.5 3.1 collective-permute-start.11
  213.9 5.1 %collective-permute-start.12 = (f32[5,1,4,1,1,256]{5,0,4,2,1,3:T(8,128)S(1)}, f32[5,1,4,1,1,256]{5,0,4,2,1,3:T(8,128)S(1)}, u32[]{:S(2)}, u32[]{:S(2)}) collective-permute-start(f32[5,1,4,1,1,256]{5,0,4,2,1,3:T(8,128)S(1)} %pad_maximum_fusion.30), channel_id=1, source_target_pairs={{0,1},{1,2},{2,3},{4,5},{5,6},{6,7},{8,9},{9,10},{10,11},{12,13},{... | collective-permute-start | bytes 61448 | tf_op jit(solution)/shard_map/ppermute | solution.py:15
  219.3 9.2 %collective-permute-start.13 = (f32[1,4,4,1,8,256]{5,0,4,2,1,3:T(1,128)S(1)}, f32[1,4,4,1,8,256]{5,0,4,2,1,3:T(1,128)S(1)}, u32[]{:S(2)}, u32[]{:S(2)}) collective-permute-start(f32[1,4,4,1,8,256]{5,0,4,2,1,3:T(1,128)S(1)} %slice.384), channel_id=1, source_target_pairs={{0,4},{4,8},{8,12},{12,16},{16,20},{20,24},{24,28},{28,0},{1,5},{5... | collective-permute-start | bytes 393224 | tf_op jit(solution)/shard_map/ppermute | solution.py:21
  221.1 51.7 %copy-start.2 = (f32[3,4,4,1,8,256]{5,0,4,2,1,3:T(4,128)}, f32[3,4,4,1,8,256]{5,0,4,2,1,3:T(4,128)S(1)}, u32[]{:S(2)}) copy-start(f32[3,4,4,1,8,256]{5,0,4,2,1,3:T(4,128)S(1)} %slice.385) | copy-start | bytes 1179652
  228.6 0.7 copy-start.6
  275.4 37.4 %copy-start.1 = (f32[4,4,4,1,8,256]{5,0,4,2,1,3:T(4,128)}, f32[4,4,4,1,8,256]{5,0,4,2,1,3:T(4,128)S(1)}, u32[]{:S(2)}) copy-start(f32[4,4,4,1,8,256]{5,0,4,2,1,3:T(4,128)S(1)} %get-tuple-element.15) | copy-start | bytes 1572868
  275.6 5.8 %collective-permute-start.14 = (f32[1,4,4,1,8,256]{5,0,4,2,1,3:T(1,128)S(1)}, f32[1,4,4,1,8,256]{5,0,4,2,1,3:T(1,128)S(1)}, u32[]{:S(2)}, u32[]{:S(2)}) collective-permute-start(f32[1,4,4,1,8,256]{5,0,4,2,1,3:T(1,128)S(1)} %slice.386), channel_id=1, source_target_pairs={{0,28},{4,0},{8,4},{12,8},{16,12},{20,16},{24,20},{28,24},{1,29},{... | collective-permute-start | bytes 393224 | tf_op jit(solution)/shard_map/ppermute | solution.py:21
  281.4 3.1 collective-permute-start.15
  298.8 5.0 %collective-permute-start.16 = (f32[5,1,4,1,1,256]{5,0,4,2,1,3:T(8,128)S(1)}, f32[5,1,4,1,1,256]{5,0,4,2,1,3:T(8,128)S(1)}, u32[]{:S(2)}, u32[]{:S(2)}) collective-permute-start(f32[5,1,4,1,1,256]{5,0,4,2,1,3:T(8,128)S(1)} %pad_maximum_fusion.28), channel_id=1, source_target_pairs={{0,1},{1,2},{2,3},{4,5},{5,6},{6,7},{8,9},{9,10},{10,11},{12,13},{... | collective-permute-start | bytes 61448 | tf_op jit(solution)/shard_map/ppermute | solution.py:15
  304.1 8.6 %collective-permute-start.17 = (f32[1,4,4,1,8,256]{5,0,4,2,1,3:T(1,128)S(1)}, f32[1,4,4,1,8,256]{5,0,4,2,1,3:T(1,128)S(1)}, u32[]{:S(2)}, u32[]{:S(2)}) collective-permute-start(f32[1,4,4,1,8,256]{5,0,4,2,1,3:T(1,128)S(1)} %slice.392), channel_id=1, source_target_pairs={{0,4},{4,8},{8,12},{12,16},{16,20},{20,24},{24,28},{28,0},{1,5},{5... | collective-permute-start | bytes 393224 | tf_op jit(solution)/shard_map/ppermute | solution.py:21
  368.6 15.8 %copy-start.5 = (f32[1,4,8,4,256,4]{4,1,2,5,3,0:T(4,128)S(1)}, f32[1,4,8,4,256,4]{4,1,2,5,3,0:T(4,128)}, u32[]{:S(2)}) copy-start(f32[1,4,8,4,256,4]{4,1,2,5,3,0:T(4,128)} %get-tuple-element.33) | copy-start | bytes 1572868
where the time goes:
time: 407 us; the launch traced here: 409 us
  blocking collectives  114 us (28%)
  local copies, waits for them, and re-layouts  111 us (27%)
  matrix products  63.2 us (16%)
  waiting for transfers between devices  52 us (13%)
  starting transfers between devices  38.9 us (10%)
  other arithmetic  18.1 us (4%)
  between operations  11.3 us (3%)
    psum x3, blocking collectives, paired_sums(): lax.psum((jnp.sum(residual * smoothed), jnp.sum(applied * smoothed)), ('g...  114 us
    reshape x4, local copies, waits for them, and re-layouts, to_blocks(): shaped = field.reshape(rows_x // 4, 4, rows_r // 4, 4, rows_y // 4, 4)  58.2 us
    ppermute x9, waiting for transfers between devices, passed_along_2(): return lax.ppermute(value, axis, pairs)  42.6 us
    reshape x2, local copies, waits for them, and re-layouts, from_blocks(): blocks.transpose(3, 0, 4, 1, 5, 2)  31.5 us
    dot_general x4, matrix products, apply_elements(): jnp.einsum('pa,pbcxyz->abcxyz', derivative, grad_x * quad_weight * metric...  23.5 us
    ppermute x9, starting transfers between devices, passed_along(): return lax.ppermute(block, axis, route)  22.1 us
    transpose x2, local copies, waits for them, and re-layouts, from_blocks(): blocks.transpose(3, 0, 4, 1, 5, 2)  18.1 us
    ppermute x9, starting transfers between devices, passed_along_2(): return lax.ppermute(value, axis, pairs)  16.8 us
  transfers between devices with their start and end apart: 18, of which 16 were waited for; matrix products, arithmetic and copies ran while one was open for 8% of the time, Pallas kernels for 0%

commit v1 on v0

v1 whole, which is shorter than its diff:
```python
import functools
import math

import jax
import jax.numpy as jnp
import numpy as np
from jax import lax
from jax.experimental import pallas as pl
from jax.experimental.pallas import tpu as pltpu
from jax.sharding import PartitionSpec as P

MESH = pl.DeviceIdType.MESH
ITERS = 3
APPLIES = ITERS + 1
CHUNK = 512
F32 = jnp.float32
BF16 = jnp.bfloat16


def gll_tables():
    root = math.sqrt(3.0 / 7.0)
    points = np.array([-1.0, -root, 0.0, root, 1.0])
    weights = np.array([0.1, 49.0 / 90.0, 32.0 / 45.0, 49.0 / 90.0, 0.1])
    factor = np.array(
        [np.prod([points[a] - points[m] for m in range(5) if m != a]) for a in range(5)]
    )
    derivative = np.zeros((5, 5))
    for p in range(5):
        for a in range(5):
            if p == a:
                derivative[p, a] = np.sum(
                    [1.0 / (points[a] - points[m]) for m in range(5) if m != a]
                )
            else:
                derivative[p, a] = factor[p] / (factor[a] * (points[p] - points[a]))
    return derivative, weights


DERIVATIVE, WEIGHTS = gll_tables()
STIFF = [[float(v) for v in row] for row in DERIVATIVE.T @ (WEIGHTS[:, None] * DERIVATIVE)]
W = [float(v) for v in WEIGHTS]


def combine(row, tiles):
    total = tiles[0] * STIFF[row][0]
    for other in range(1, 4):
        total = total + tiles[other] * STIFF[row][other]
    return total


def exact_pieces(value):
    high = value.astype(BF16)
    rest = value - high.astype(F32)
    middle = rest.astype(BF16)
    low = (rest - middle.astype(F32)).astype(BF16)
    return high, middle, low


def dot(left, right):
    return jnp.dot(left, right, preferred_element_type=F32)


def one_where(condition):
    return jnp.where(condition, 1.0, 0.0).astype(BF16)


def kernel(
    n_group, n_rad, source_hbm, guess_hbm, metric_hbm, sol_hbm, res_hbm,
    source_in, guess_in, own, prev, below, diag,
    c0, c0p, c1, c1s, c2, c2s, inv,
    x, r, u, w, m_first, m_second, n, z, s, p,
    plane_out, plane_in, part_in, row_out, row_in, rowpart_out, rowpart_in,
    rad_out, rad_in, group_out, group_in,
    local_sem, met_send, met_recv, halo_send, halo_recv,
    rad_send, rad_recv, group_send, group_recv,
):
    e = lax.axis_index("group")
    k = lax.axis_index("rad")
    nxt, prv = lax.rem(e + 1, n_group), lax.rem(e + n_group - 1, n_group)
    up, down = lax.rem(k + 1, n_rad), lax.rem(k + n_rad - 1, n_rad)
    has_below = jnp.where(k == 0, 0.0, 1.0).astype(F32)
    has_above = jnp.where(k == n_rad - 1, 0.0, 1.0).astype(F32)
    rows, width = own.shape[1:]
    nodes, lanes = 16 * rows, 4 * width
    last = rows - 1

    loads = [
        pltpu.make_async_copy(metric_hbm, own, local_sem.at[0]),
        pltpu.make_async_copy(guess_hbm, guess_in, local_sem.at[1]),
        pltpu.make_async_copy(source_hbm, source_in, local_sem.at[2]),
    ]
    for load in loads:
        load.start()

    barrier = pltpu.get_barrier_semaphore()
    for d in range(1, n_group):
        pl.semaphore_signal(
            barrier, inc=1, device_id=(lax.rem(e + d, n_group), k), device_id_type=MESH
        )
    for d in range(1, n_rad):
        pl.semaphore_signal(
            barrier, inc=1, device_id=(e, lax.rem(k + d, n_rad)), device_id_type=MESH
        )
    pl.semaphore_signal(barrier, inc=1, device_id=(nxt, up), device_id_type=MESH)
    pl.semaphore_signal(barrier, inc=1, device_id=(prv, down), device_id_type=MESH)

    i0 = lax.broadcasted_iota(jnp.int32, (CHUNK, CHUNK), 0)
    i1 = lax.broadcasted_iota(jnp.int32, (CHUNK, CHUNK), 1)
    part = CHUNK // 4
    lane_split = one_where(i0 == 4 * (i1 % part) + i1 // part)
    r0 = lax.broadcasted_iota(jnp.int32, (nodes, nodes), 0)
    r1 = lax.broadcasted_iota(jnp.int32, (nodes, nodes), 1)
    block = 4 * rows

    def split_row(i):
        return (i // block) * block + 4 * (i % rows) + (i % block) // rows

    row_split = one_where(r1 == split_row(r0))

    def to_blocks(field_in, target):
        pieces = exact_pieces(field_in[...].reshape(nodes, lanes))
        pieces = [dot(row_split, piece).astype(BF16) for piece in pieces]
        for h in range(lanes // CHUNK):
            cut = slice(h * CHUNK, (h + 1) * CHUNK)
            moved = dot(pieces[0][:, cut], lane_split)
            moved = moved + dot(pieces[1][:, cut], lane_split)
            moved = moved + dot(pieces[2][:, cut], lane_split)
            moved = moved.reshape(4, 4, rows, CHUNK)
            for c in range(4):
                target[:, :, c, :, h * part:(h + 1) * part] = (
                    moved[:, :, :, c * part:(c + 1) * part]
                )

    pl.semaphore_wait(barrier, n_group + n_rad)

    def remote(src, dst, send, recv, where):
        return pltpu.make_async_remote_copy(
            src_ref=src, dst_ref=dst, send_sem=send, recv_sem=recv,
            device_id=where, device_id_type=MESH,
        )

    loads[0].wait()
    metric_moves = [
        remote(own, prev, met_send.at[0], met_recv.at[0], (nxt, k)),
        remote(own, below, met_send.at[1], met_recv.at[1], (e, up)),
        remote(own, diag, met_send.at[2], met_recv.at[2], (nxt, up)),
    ]
    for move in metric_moves:
        move.start()

    loads[1].wait()
    to_blocks(guess_in, x)

    row_index = lax.broadcasted_iota(jnp.int32, (rows, width), 0)
    first_row, last_row = row_index == 0, row_index == last

    def shift_y(tile):
        return pltpu.roll(tile, 1, 1)

    def next_y(tile):
        return pltpu.roll(tile, width - 1, 1)

    def moves_of(j, v):
        return [
            remote(v.at[0], plane_in.at[j], halo_send.at[j, 0], halo_recv.at[j, 0], (prv, k)),
            remote(row_out.at[j], row_in.at[j], halo_send.at[j, 1], halo_recv.at[j, 1], (e, down)),
            remote(rowpart_out.at[j], rowpart_in.at[j], halo_send.at[j, 2], halo_recv.at[j, 2], (e, up)),
            remote(plane_out.at[j], part_in.at[j], halo_send.at[j, 3], halo_recv.at[j, 3], (nxt, k)),
        ]

    def looped(body):
        def step(i, carry):
            body(i)
            return carry

        lax.fori_loop(0, 4, step, 0)

    def start_plane(j, v):
        moves_of(j, v)[0].start()

    def start_rest(j, v):
        moves = moves_of(j, v)

        def plane(b):
            for c in range(4):
                plane_out[j, b, c] = c0[b, c] * combine(4, [v[a, b, c] for a in range(4)])

        looped(plane)
        moves[3].start()

        def edge(a):
            for c in range(4):
                row_out[j, a, pl.ds(c, 1), :] = v[a, 0, c, pl.ds(0, 1), :]
                rowpart_out[j, a, pl.ds(c, 1), :] = c1[a, c, pl.ds(last, 1), :] * combine(
                    4, [v[a, b, c, pl.ds(last, 1), :] for b in range(4)]
                )

        looped(edge)
        moves[1].start()
        moves[2].start()

    def local_part(v, out):
        def along_x(b):
            for c in range(4):
                tiles = [v[a, b, c] for a in range(4)]
                scale = c0[b, c]
                out[0, b, c] = scale * combine(0, tiles) + c0p[b, c] * tiles[0]
                for a in range(1, 4):
                    out[a, b, c] = scale * combine(a, tiles)

        looped(along_x)

        def along_r(a):
            for c in range(4):
                tiles = [v[a, b, c] for b in range(4)]
                scale = c1[a, c]
                above = jnp.where(last_row, 0.0, pltpu.roll(tiles[0], rows - 1, 0))
                carried = jnp.where(first_row, 0.0, pltpu.roll(scale * combine(4, tiles), 1, 0))
                for b in range(4):
                    value = scale * (combine(b, tiles) + above * STIFF[b][4])
                    if b == 0:
                        value = value + carried + c1s[a, c] * tiles[0]
                    out[a, b, c] += value

        looped(along_r)

        def along_y(a):
            for b in range(4):
                tiles = [v[a, b, c] for c in range(4)]
                scale = c2[a, b]
                above = next_y(tiles[0])
                carried = shift_y(scale * combine(4, tiles))
                for c in range(4):
                    value = scale * (combine(c, tiles) + above * STIFF[c][4])
                    if c == 0:
                        value = value + carried + c2s[a, b] * tiles[0]
                    out[a, b, c] += value

        looped(along_y)

    def finish(j, v, out):
        moves = moves_of(j, v)
        moves[1].wait()
        moves[2].wait()

        def edge(a):
            for c in range(4):
                above = (has_above * row_in[j, a, pl.ds(c, 1), :]) * c1[a, c, pl.ds(last, 1), :]
                for b in range(4):
                    out[a, b, c, pl.ds(last, 1), :] += above * STIFF[b][4]
                out[a, 0, c, pl.ds(0, 1), :] += has_below * rowpart_in[j, a, pl.ds(c, 1), :]

        looped(edge)
        moves[0].wait()
        moves[3].wait()

        def plane(b):
            for c in range(4):
                above = c0[b, c] * plane_in[j, b, c]
                out[0, b, c] += above * STIFF[0][4] + part_in[j, b, c]
                for a in range(1, 4):
                    out[a, b, c] += above * STIFF[a][4]

        looped(plane)

    start_plane(0, x)
    for move in metric_moves:
        move.wait()

    def lower(tile, tile_below):
        edge_row = has_below * tile_below[last:, :]
        return jnp.where(first_row, edge_row, pltpu.roll(tile, 1, 0))

    def four(plain, other, along):
        both = plain + other
        return {
            (0, 0): plain, (1, 0): both,
            (0, 1): plain + along(plain), (1, 1): both + along(both),
        }

    def pick(table, first, second):
        scale = W[first] * W[second]
        return table[(int(first == 0), int(second == 0))] * scale

    own_0, own_1, own_2 = own[0], own[1], own[2]
    prev_0, prev_1, prev_2 = prev[0], prev[1], prev[2]
    below_0, below_1, below_2 = below[0], below[1], below[2]
    diag_0, diag_1, diag_2 = diag[0], diag[1], diag[2]
    table_0 = four(own_0, lower(own_0, below_0), shift_y)
    table_0p = four(prev_0, lower(prev_0, diag_0), shift_y)
    table_1 = four(own_1, prev_1, shift_y)
    table_1b = four(below_1, diag_1, shift_y)
    lower_2, lower_2p = lower(own_2, below_2), lower(prev_2, diag_2)
    table_2 = {
        (0, 0): own_2, (0, 1): own_2 + lower_2,
        (1, 0): own_2 + prev_2, (1, 1): own_2 + lower_2 + prev_2 + lower_2p,
    }
    for i in range(4):
        for j in range(4):
            c0[i, j] = pick(table_0, i, j)
            c0p[i, j] = pick(table_0p, i, j) * STIFF[4][4]
            line = pick(table_1, i, j)
            c1[i, j] = line
            c1s[i, j] = lower(line, pick(table_1b, i, j)) * STIFF[4][4]
            line = pick(table_2, i, j)
            c2[i, j] = line
            c2s[i, j] = shift_y(line) * STIFF[4][4]

    start_rest(0, x)
    loads[2].wait()
    to_blocks(source_in, r)

    def diagonal(a):
        for b in range(4):
            for c in range(4):
                zero_a = jnp.where(a == 0, 1.0, 0.0).astype(F32)
                middle = jnp.where(a == 2, STIFF[2][2], STIFF[1][1]).astype(F32)
                stiff = jnp.where(a == 0, STIFF[0][0], middle).astype(F32)
                total = c0[b, c] * stiff + c0p[b, c] * zero_a
                total = total + c1[a, c] * STIFF[b][b]
                total = total + c2[a, b] * STIFF[c][c]
                if b == 0:
                    total = total + c1s[a, c]
                if c == 0:
                    total = total + c2s[a, b]
                inv[a, b, c] = 1.0 / total

    looped(diagonal)
    local_part(x, n)
    finish(0, x, n)

    def initial(a):
        for b in range(4):
            for c in range(4):
                residual = r[a, b, c] - n[a, b, c]
                r[a, b, c] = residual
                u[a, b, c] = inv[a, b, c] * residual

    looped(initial)

    start_plane(1, u)
    start_rest(1, u)
    local_part(u, w)
    finish(1, u, w)

    def rad_moves(t):
        return [
            remote(rad_out.at[t], rad_in.at[t, d - 1], rad_send.at[t, d - 1],
                   rad_recv.at[t, d - 1], (e, lax.rem(k + d, n_rad)))
            for d in range(1, n_rad)
        ]

    def group_moves(t):
        return [
            remote(group_out.at[t], group_in.at[t, d - 1], group_send.at[t, d - 1],
                   group_recv.at[t, d - 1], (lax.rem(e + d, n_group), k))
            for d in range(1, n_group)
        ]

    def lane_sum(tile):
        row = jnp.sum(tile, axis=0, keepdims=True)
        total = row[:, :128]
        for h in range(1, width // 128):
            total = total + row[:, h * 128:(h + 1) * 128]
        return total

    def sums_begin(t, gamma_tile, delta_tile):
        index = lax.broadcasted_iota(jnp.int32, (8, 128), 0)
        rad_out[t] = jnp.where(
            index == 0, lane_sum(gamma_tile), jnp.where(index == 1, lane_sum(delta_tile), 0.0)
        )
        for move in rad_moves(t):
            move.start()

    def sums_middle(t):
        total = rad_out[t]
        for d, move in enumerate(rad_moves(t)):
            move.wait()
            total = total + rad_in[t, d]
        group_out[t] = total
        for move in group_moves(t):
            move.start()

    def sums_end(t):
        total = group_out[t]
        for d, move in enumerate(group_moves(t)):
            move.wait()
            total = total + group_in[t, d]
        total = jnp.sum(total, axis=1, keepdims=True)
        return total[0:1, :], total[1:2, :]

    def carried_loop(body):
        zero = jnp.zeros((rows, width), F32)
        return lax.fori_loop(0, 4, body, (zero, zero))

    def first_sums(a, carry):
        gamma, delta = carry
        for b in range(4):
            for c in range(4):
                value, applied = u[a, b, c], w[a, b, c]
                gamma = gamma + r[a, b, c] * value
                delta = delta + applied * value
                m_first[a, b, c] = inv[a, b, c] * applied
        return gamma, delta

    tiles = carried_loop(first_sums)
    sums_begin(0, *tiles)
    start_plane(2, m_first)
    start_rest(2, m_first)
    sums_middle(0)
    local_part(m_first, z)
    finish(2, m_first, z)
    gamma_0, delta_0 = sums_end(0)
    alpha_0 = gamma_0 / delta_0
    step = jnp.broadcast_to(alpha_0, (rows, width))

    def first_update(a, carry):
        gamma, delta = carry
        for b in range(4):
            for c in range(4):
                applied, search = w[a, b, c], u[a, b, c]
                s[a, b, c] = applied
                p[a, b, c] = search
                x[a, b, c] += step * search
                residual = r[a, b, c] - step * applied
                r[a, b, c] = residual
                scale = inv[a, b, c]
                smooth = scale * residual
                u[a, b, c] = smooth
                applied = applied - step * z[a, b, c]
                w[a, b, c] = applied
                m_second[a, b, c] = scale * applied
                gamma = gamma + residual * smooth
                delta = delta + applied * smooth
        return gamma, delta

    tiles = carried_loop(first_update)
    sums_begin(1, *tiles)
    start_plane(3, m_second)
    start_rest(3, m_second)
    sums_middle(1)
    local_part(m_second, n)
    finish(3, m_second, n)
    gamma_1, delta_1 = sums_end(1)
    beta_0 = gamma_1 / gamma_0
    alpha_1 = gamma_1 / (delta_1 - beta_0 * gamma_1 / alpha_0)
    step_1 = jnp.broadcast_to(alpha_1, (rows, width))
    ratio_1 = jnp.broadcast_to(beta_0, (rows, width))

    def second_update(a, carry):
        gamma, delta = carry
        for b in range(4):
            for c in range(4):
                applied = w[a, b, c]
                searched = applied + ratio_1 * s[a, b, c]
                s[a, b, c] = searched
                search = u[a, b, c] + ratio_1 * p[a, b, c]
                p[a, b, c] = search
                x[a, b, c] += step_1 * search
                residual = r[a, b, c] - step_1 * searched
                r[a, b, c] = residual
                smooth = inv[a, b, c] * residual
                u[a, b, c] = smooth
                applied = applied - step_1 * (n[a, b, c] + ratio_1 * z[a, b, c])
                w[a, b, c] = applied
                gamma = gamma + residual * smooth
                delta = delta + applied * smooth
        return gamma, delta

    tiles = carried_loop(second_update)
    sums_begin(2, *tiles)
    sums_middle(2)
    lane_join = one_where(i1 == 4 * (i0 % part) + i0 // part)
    row_join = one_where(r0 == split_row(r1))
    gamma_2, delta_2 = sums_end(2)
    beta_1 = gamma_2 / gamma_1
    alpha_2 = gamma_2 / (delta_2 - beta_1 * gamma_2 / alpha_1)
    step_2 = jnp.broadcast_to(alpha_2, (rows, width))
    ratio_2 = jnp.broadcast_to(beta_1, (rows, width))

    def last_update(a):
        for b in range(4):
            for c in range(4):
                x[a, b, c] += step_2 * (u[a, b, c] + ratio_2 * p[a, b, c])
                r[a, b, c] -= step_2 * (w[a, b, c] + ratio_2 * s[a, b, c])

    looped(last_update)

    def from_blocks(field, target):
        for h in range(lanes // CHUNK):
            wide = jnp.concatenate(
                [field[:, :, c, :, h * part:(h + 1) * part] for c in range(4)], axis=-1
            ).reshape(nodes, CHUNK)
            total = None
            for piece in exact_pieces(wide):
                moved = dot(piece, lane_join).astype(BF16)
                moved = dot(row_join, moved)
                total = moved if total is None else total + moved
            target[:, :, h * CHUNK:(h + 1) * CHUNK] = total.reshape(4, block, CHUNK)

    from_blocks(x, guess_in)
    store_x = pltpu.make_async_copy(guess_in, sol_hbm, local_sem.at[3])
    store_x.start()
    from_blocks(r, source_in)
    store_r = pltpu.make_async_copy(source_in, res_hbm, local_sem.at[4])
    store_r.start()
    store_x.wait()
    store_r.wait()


def solution(mesh):
    n_group, n_rad = mesh.shape["group"], mesh.shape["rad"]

    def local(source_term, initial_guess, metric):
        shape = source_term.shape
        metric = metric.reshape(3, metric.shape[2], metric.shape[3])
        rows, width = metric.shape[1:]
        assert shape == (4, 4 * rows, 4 * width) and rows % 8 == 0 and shape[2] % CHUNK == 0
        tile = (rows, width)
        field = pltpu.VMEM((4, 4, 4) + tile, F32)
        plane = pltpu.VMEM((4, 4) + tile, F32)
        planes = pltpu.VMEM((APPLIES, 4, 4) + tile, F32)
        edges = pltpu.VMEM((APPLIES, 4, 4, width), F32)
        any_space = pl.BlockSpec(memory_space=pl.ANY)
        return pl.pallas_call(
            functools.partial(kernel, n_group, n_rad),
            out_shape=[jax.ShapeDtypeStruct(shape, F32)] * 2,
            in_specs=[any_space] * 3,
            out_specs=[any_space] * 2,
            scratch_shapes=[
                pltpu.VMEM(shape, F32), pltpu.VMEM(shape, F32),
                *[pltpu.VMEM((3,) + tile, F32)] * 4,
                *[plane] * 6, field,
                *[field] * 10,
                planes, planes, planes, edges, edges, edges, edges,
                pltpu.VMEM((ITERS, 8, 128), F32), pltpu.VMEM((ITERS, n_rad - 1, 8, 128), F32),
                pltpu.VMEM((ITERS, 8, 128), F32), pltpu.VMEM((ITERS, n_group - 1, 8, 128), F32),
                pltpu.SemaphoreType.DMA((5,)),
                pltpu.SemaphoreType.DMA((3,)), pltpu.SemaphoreType.DMA((3,)),
                pltpu.SemaphoreType.DMA((APPLIES, 4)), pltpu.SemaphoreType.DMA((APPLIES, 4)),
                pltpu.SemaphoreType.DMA((ITERS, n_rad - 1)), pltpu.SemaphoreType.DMA((ITERS, n_rad - 1)),
                pltpu.SemaphoreType.DMA((ITERS, n_group - 1)), pltpu.SemaphoreType.DMA((ITERS, n_group - 1)),
            ],
            compiler_params=pltpu.CompilerParams(
                collective_id=0, has_side_effects=True, vmem_limit_bytes=40 * 1024 * 1024
            ),
            name="pcg",
        )(source_term, initial_guess, metric)

    in_specs = (P("group", "rad", None), P("group", "rad", None), P(None, "group", "rad", None))
    out_specs = (P("group", "rad", None), P("group", "rad", None))
    return jax.shard_map(local, mesh=mesh, in_specs=in_specs, out_specs=out_specs, check_vma=False)
```

time: 407 us -> 55 us (0.14)
  blocking collectives: 114 us -> 0 us
  local copies, waits for them, and re-layouts: 111 us -> 4.4 us
  matrix products: 63.2 us -> 0 us
  waiting for transfers between devices: 52 us -> 0 us
  Pallas kernels: 0 us -> 49.7 us
  starting transfers between devices: 38.9 us -> 0 us
  other arithmetic: 18.1 us -> 0 us
  between operations: 11.3 us -> 0.65 us
    psum x3 -> x0, blocking collectives: 114 us -> none  [paired_sums(): lax.psum((jnp.sum(residual * smoothed), jnp.sum(applied * smoothed)), ('g...]
    reshape x6 -> x0, local copies, waits for them, and re-layouts: 89.7 us -> none  [the longest x4 58.2 us: to_blocks(): shaped = field.reshape(rows_x // 4, 4, rows_r // 4, 4, rows_y // 4, 4)]
    dot_general x24 -> x0, matrix products: 63.2 us -> none  [the longest x4 23.5 us: apply_elements(): jnp.einsum('pa,pbcxyz->abcxyz', derivative, grad_x * quad_weight * metric...]
    ppermute x18 -> x0, waiting for transfers between devices: 52 us -> none  [the longest x9 42.6 us: passed_along_2(): return lax.ppermute(value, axis, pairs)]
    pallas_call x0 -> x1, Pallas kernels: none -> 49.7 us  [local(): pl.pallas_call(functools.partial(kernel, n_group, n_rad), out_shape=[jax....]
    ppermute x18 -> x0, starting transfers between devices: 38.9 us -> none  [the longest x9 22.1 us: passed_along(): return lax.ppermute(block, axis, route)]
    transpose x2 -> x0, local copies, waits for them, and re-layouts: 18.1 us -> none  [from_blocks(): blocks.transpose(3, 0, 4, 1, 5, 2)]
    another operation x7 -> x0, other arithmetic: 4.38 us -> none
  transfers between devices with their start and end apart: 18 -> 0, of which waited for: 16 -> 0; matrix products, arithmetic and copies ran while one was open for 8% -> 0% of each run, Pallas kernels for 0% -> 0%
where the time goes in v1:
time: 55 us; the launch traced here: 54.7 us
  Pallas kernels  49.7 us (90%)
  local copies, waits for them, and re-layouts  4.4 us (8%)
  between operations  0.65 us (1%)
    pallas_call x1, Pallas kernels, local(): pl.pallas_call(functools.partial(kernel, n_group, n_rad), out_shape=[jax....  49.7 us
    unnamed x8, local copies, waits for them, and re-layouts  4.4 us

profile of v1, /device:TPU:0, one launch (start us, length us, event | category | flops | bytes accessed | tf_op | source)
XLA Modules:
  0.0 54.7 jit_solution(5934774092161567774)
XLA Ops:
  0.6 0.0 copy-start
  0.6 1.0 %copy-done = f32[4,32,1024]{2,1,0:T(8,128)S(1)} copy-done((f32[4,32,1024]{2,1,0:T(8,128)S(1)}, f32[4,32,1024]{2,1,0:T(8,128)}, u32[]{:S(2)}) %copy-start) | copy-done | bytes 524312
  1.7 0.0 copy-start.1
  1.7 1.0 %copy-done.1 = f32[4,32,1024]{2,1,0:T(8,128)S(1)} copy-done((f32[4,32,1024]{2,1,0:T(8,128)S(1)}, f32[4,32,1024]{2,1,0:T(8,128)}, u32[]{:S(2)}) %copy-start.1) | copy-done | bytes 524312
  2.7 0.0 copy-start.2
  2.7 0.7 %copy-done.2 = f32[3,1,8,256]{3,2,1,0:T(8,128)S(1)} copy-done((f32[3,1,8,256]{3,2,1,0:T(8,128)S(1)}, f32[3,1,8,256]{3,2,1,0:T(8,128)}, u32[]{:S(2)}) %copy-start.2) | copy-done | bytes 24600
  3.5 49.7 %pcg.1 = (f32[4,32,1024]{2,1,0:T(8,128)S(1)}, f32[4,32,1024]{2,1,0:T(8,128)S(1)}) custom-call(f32[4,32,1024]{2,1,0:T(8,128)S(1)} %copy-done, f32[4,32,1024]{2,1,0:T(8,128)S(1)} %copy-done.1, f32[3,8,256]{2,1,0:T(8,128)S(1)} %bitcast.1), custom_call_target="tpu_custom_call" | custom-call | tf_op jit(solution)/shard_map/pcg/pallas_call | solution.py:525
  53.1 0.8 %copy.7 = f32[4,32,1024]{2,1,0:T(8,128)} copy(f32[4,32,1024]{2,1,0:T(8,128)S(1)} %get-tuple-element.4) | data formatting | bytes 1048576
  53.9 0.8 %copy.8 = f32[4,32,1024]{2,1,0:T(8,128)} copy(f32[4,32,1024]{2,1,0:T(8,128)S(1)} %get-tuple-element.5) | data formatting | bytes 1048576
Async XLA Ops:
  0.6 1.0 %copy-start = (f32[4,32,1024]{2,1,0:T(8,128)S(1)}, f32[4,32,1024]{2,1,0:T(8,128)}, u32[]{:S(2)}) copy-start(f32[4,32,1024]{2,1,0:T(8,128)} %source_hbm.1) | copy-start | bytes 1572868
  1.7 1.0 %copy-start.1 = (f32[4,32,1024]{2,1,0:T(8,128)S(1)}, f32[4,32,1024]{2,1,0:T(8,128)}, u32[]{:S(2)}) copy-start(f32[4,32,1024]{2,1,0:T(8,128)} %guess_hbm.1) | copy-start | bytes 1572868
  2.7 0.7 %copy-start.2 = (f32[3,1,8,256]{3,2,1,0:T(8,128)S(1)}, f32[3,1,8,256]{3,2,1,0:T(8,128)}, u32[]{:S(2)}) copy-start(f32[3,1,8,256]{3,2,1,0:T(8,128)} %param.5) | copy-start | bytes 73732

commit v2 on v1

--- a/solution.py
+++ b/solution.py
@@ -71,7 +71,7 @@
     x, r, u, w, m_first, m_second, n, z, s, p,
     plane_out, plane_in, part_in, row_out, row_in, rowpart_out, rowpart_in,
     rad_out, rad_in, group_out, group_in,
-    local_sem, met_send, met_recv, halo_send, halo_recv,
+    local_sem, met_send, met_recv, halo_send, halo_recv, row_send, row_recv,
     rad_send, rad_recv, group_send, group_recv,
 ):
     e = lax.axis_index("group")
@@ -160,12 +160,20 @@
     def next_y(tile):
         return pltpu.roll(tile, width - 1, 1)
 
-    def moves_of(j, v):
+    def plane_move(j, b, v):
+        return remote(
+            v.at[0, b], plane_in.at[j, b], halo_send.at[j, b, 0], halo_recv.at[j, b, 0], (prv, k)
+        )
+
+    def part_move(j, b):
+        return remote(
+            plane_out.at[j, b], part_in.at[j, b], halo_send.at[j, b, 1], halo_recv.at[j, b, 1], (nxt, k)
+        )
+
+    def row_moves(j):
         return [
-            remote(v.at[0], plane_in.at[j], halo_send.at[j, 0], halo_recv.at[j, 0], (prv, k)),
-            remote(row_out.at[j], row_in.at[j], halo_send.at[j, 1], halo_recv.at[j, 1], (e, down)),
-            remote(rowpart_out.at[j], rowpart_in.at[j], halo_send.at[j, 2], halo_recv.at[j, 2], (e, up)),
-            remote(plane_out.at[j], part_in.at[j], halo_send.at[j, 3], halo_recv.at[j, 3], (nxt, k)),
+            remote(row_out.at[j], row_in.at[j], row_send.at[j, 0], row_recv.at[j, 0], (e, down)),
+            remote(rowpart_out.at[j], rowpart_in.at[j], row_send.at[j, 1], row_recv.at[j, 1], (e, up)),
         ]
 
     def looped(body):
@@ -175,19 +183,7 @@
 
         lax.fori_loop(0, 4, step, 0)
 
-    def start_plane(j, v):
-        moves_of(j, v)[0].start()
-
-    def start_rest(j, v):
-        moves = moves_of(j, v)
-
-        def plane(b):
-            for c in range(4):
-                plane_out[j, b, c] = c0[b, c] * combine(4, [v[a, b, c] for a in range(4)])
-
-        looped(plane)
-        moves[3].start()
-
+    def start_rows(j, v):
         def edge(a):
             for c in range(4):
                 row_out[j, a, pl.ds(c, 1), :] = v[a, 0, c, pl.ds(0, 1), :]
@@ -196,10 +192,10 @@
                 )
 
         looped(edge)
-        moves[1].start()
-        moves[2].start()
-
-    def local_part(v, out):
+        for move in row_moves(j):
+            move.start()
+
+    def local_part(v, out, between=None):
         def along_x(b):
             for c in range(4):
                 tiles = [v[a, b, c] for a in range(4)]
@@ -209,20 +205,6 @@
                     out[a, b, c] = scale * combine(a, tiles)
 
         looped(along_x)
-
-        def along_r(a):
-            for c in range(4):
-                tiles = [v[a, b, c] for b in range(4)]
-                scale = c1[a, c]
-                above = jnp.where(last_row, 0.0, pltpu.roll(tiles[0], rows - 1, 0))
-                carried = jnp.where(first_row, 0.0, pltpu.roll(scale * combine(4, tiles), 1, 0))
-                for b in range(4):
-                    value = scale * (combine(b, tiles) + above * STIFF[b][4])
-                    if b == 0:
-                        value = value + carried + c1s[a, c] * tiles[0]
-                    out[a, b, c] += value
-
-        looped(along_r)
 
         def along_y(a):
             for b in range(4):
@@ -237,11 +219,26 @@
                     out[a, b, c] += value
 
         looped(along_y)
-
-    def finish(j, v, out):
-        moves = moves_of(j, v)
-        moves[1].wait()
-        moves[2].wait()
+        if between is not None:
+            between()
+
+        def along_r(a):
+            for c in range(4):
+                tiles = [v[a, b, c] for b in range(4)]
+                scale = c1[a, c]
+                above = jnp.where(last_row, 0.0, pltpu.roll(tiles[0], rows - 1, 0))
+                carried = jnp.where(first_row, 0.0, pltpu.roll(scale * combine(4, tiles), 1, 0))
+                for b in range(4):
+                    value = scale * (combine(b, tiles) + above * STIFF[b][4])
+                    if b == 0:
+                        value = value + carried + c1s[a, c] * tiles[0]
+                    out[a, b, c] += value
+
+        looped(along_r)
+
+    def finish_rows(j, out):
+        for move in row_moves(j):
+            move.wait()
 
         def edge(a):
             for c in range(4):
@@ -251,21 +248,34 @@
                 out[a, 0, c, pl.ds(0, 1), :] += has_below * rowpart_in[j, a, pl.ds(c, 1), :]
 
         looped(edge)
-        moves[0].wait()
-        moves[3].wait()
-
-        def plane(b):
+
+    def streamed(j, v, out, update, following=None, sums=False):
+        def quarter(b, carry):
+            plane_move(j, b, v).wait()
+            part_move(j, b).wait()
             for c in range(4):
                 above = c0[b, c] * plane_in[j, b, c]
-                out[0, b, c] += above * STIFF[0][4] + part_in[j, b, c]
-                for a in range(1, 4):
-                    out[a, b, c] += above * STIFF[a][4]
-
-        looped(plane)
-
-    start_plane(0, x)
-    for move in metric_moves:
-        move.wait()
+                tiles = []
+                for a in range(4):
+                    applied = out[a, b, c] + above * STIFF[a][4]
+                    if a == 0:
+                        applied = applied + part_in[j, b, c]
+                    tile, terms = update(a, b, c, applied)
+                    tiles.append(tile)
+                    if sums:
+                        carry = (carry[0] + terms[0], carry[1] + terms[1])
+                if following is not None:
+                    plane_out[j + 1, b, c] = c0[b, c] * combine(4, tiles)
+            if following is not None:
+                part_move(j + 1, b).start()
+                plane_move(j + 1, b, following).start()
+            return carry
+
+        zero = jnp.zeros((rows, width), F32)
+        return lax.fori_loop(0, 4, quarter, (zero, zero) if sums else 0)
+
+    looped(lambda b: plane_move(0, b, x).start())
+    metric_moves[1].wait()
 
     def lower(tile, tile_below):
         edge_row = has_below * tile_below[last:, :]
@@ -282,11 +292,23 @@
         scale = W[first] * W[second]
         return table[(int(first == 0), int(second == 0))] * scale
 
-    own_0, own_1, own_2 = own[0], own[1], own[2]
+    table_0 = four(own[0], lower(own[0], below[0]), shift_y)
+    for i in range(4):
+        for j in range(4):
+            c0[i, j] = pick(table_0, i, j)
+
+    def first_planes(b):
+        for c in range(4):
+            plane_out[0, b, c] = c0[b, c] * combine(4, [x[a, b, c] for a in range(4)])
+        part_move(0, b).start()
+
+    looped(first_planes)
+    metric_moves[0].wait()
+    metric_moves[2].wait()
+    own_1, own_2 = own[1], own[2]
     prev_0, prev_1, prev_2 = prev[0], prev[1], prev[2]
-    below_0, below_1, below_2 = below[0], below[1], below[2]
+    below_1, below_2 = below[1], below[2]
     diag_0, diag_1, diag_2 = diag[0], diag[1], diag[2]
-    table_0 = four(own_0, lower(own_0, below_0), shift_y)
     table_0p = four(prev_0, lower(prev_0, diag_0), shift_y)
     table_1 = four(own_1, prev_1, shift_y)
     table_1b = four(below_1, diag_1, shift_y)
@@ -297,7 +319,6 @@
     }
     for i in range(4):
         for j in range(4):
-            c0[i, j] = pick(table_0, i, j)
             c0p[i, j] = pick(table_0p, i, j) * STIFF[4][4]
             line = pick(table_1, i, j)
             c1[i, j] = line
@@ -306,7 +327,7 @@
             c2[i, j] = line
             c2s[i, j] = shift_y(line) * STIFF[4][4]
 
-    start_rest(0, x)
+    start_rows(0, x)
     loads[2].wait()
     to_blocks(source_in, r)
 
@@ -326,23 +347,6 @@
                 inv[a, b, c] = 1.0 / total
 
     looped(diagonal)
-    local_part(x, n)
-    finish(0, x, n)
-
-    def initial(a):
-        for b in range(4):
-            for c in range(4):
-                residual = r[a, b, c] - n[a, b, c]
-                r[a, b, c] = residual
-                u[a, b, c] = inv[a, b, c] * residual
-
-    looped(initial)
-
-    start_plane(1, u)
-    start_rest(1, u)
-    local_part(u, w)
-    finish(1, u, w)
-
     def rad_moves(t):
         return [
             remote(rad_out.at[t], rad_in.at[t, d - 1], rad_send.at[t, d - 1],
@@ -389,85 +393,81 @@
         total = jnp.sum(total, axis=1, keepdims=True)
         return total[0:1, :], total[1:2, :]
 
-    def carried_loop(body):
-        zero = jnp.zeros((rows, width), F32)
-        return lax.fori_loop(0, 4, body, (zero, zero))
-
-    def first_sums(a, carry):
-        gamma, delta = carry
-        for b in range(4):
-            for c in range(4):
-                value, applied = u[a, b, c], w[a, b, c]
-                gamma = gamma + r[a, b, c] * value
-                delta = delta + applied * value
-                m_first[a, b, c] = inv[a, b, c] * applied
-        return gamma, delta
-
-    tiles = carried_loop(first_sums)
+    local_part(x, n)
+    finish_rows(0, n)
+
+    def initial(a, b, c, applied):
+        residual = r[a, b, c] - applied
+        r[a, b, c] = residual
+        smooth = inv[a, b, c] * residual
+        u[a, b, c] = smooth
+        return smooth, None
+
+    streamed(0, x, n, initial, u)
+    start_rows(1, u)
+    local_part(u, w)
+    finish_rows(1, w)
+
+    def first_sums(a, b, c, applied):
+        w[a, b, c] = applied
+        value = u[a, b, c]
+        smooth = inv[a, b, c] * applied
+        m_first[a, b, c] = smooth
+        return smooth, (r[a, b, c] * value, applied * value)
+
+    tiles = streamed(1, u, w, first_sums, m_first, True)
     sums_begin(0, *tiles)
-    start_plane(2, m_first)
-    start_rest(2, m_first)
-    sums_middle(0)
-    local_part(m_first, z)
-    finish(2, m_first, z)
+    start_rows(2, m_first)
+    local_part(m_first, z, lambda: sums_middle(0))
+    finish_rows(2, z)
     gamma_0, delta_0 = sums_end(0)
     alpha_0 = gamma_0 / delta_0
     step = jnp.broadcast_to(alpha_0, (rows, width))
 
-    def first_update(a, carry):
-        gamma, delta = carry
-        for b in range(4):
-            for c in range(4):
-                applied, search = w[a, b, c], u[a, b, c]
-                s[a, b, c] = applied
-                p[a, b, c] = search
-                x[a, b, c] += step * search
-                residual = r[a, b, c] - step * applied
-                r[a, b, c] = residual
-                scale = inv[a, b, c]
-                smooth = scale * residual
-                u[a, b, c] = smooth
-                applied = applied - step * z[a, b, c]
-                w[a, b, c] = applied
-                m_second[a, b, c] = scale * applied
-                gamma = gamma + residual * smooth
-                delta = delta + applied * smooth
-        return gamma, delta
-
-    tiles = carried_loop(first_update)
+    def first_update(a, b, c, powered):
+        z[a, b, c] = powered
+        applied, search = w[a, b, c], u[a, b, c]
+        s[a, b, c] = applied
+        p[a, b, c] = search
+        x[a, b, c] += step * search
+        residual = r[a, b, c] - step * applied
+        r[a, b, c] = residual
+        scale = inv[a, b, c]
+        smooth = scale * residual
+        u[a, b, c] = smooth
+        applied = applied - step * powered
+        w[a, b, c] = applied
+        powered = scale * applied
+        m_second[a, b, c] = powered
+        return powered, (residual * smooth, applied * smooth)
+
+    tiles = streamed(2, m_first, z, first_update, m_second, True)
     sums_begin(1, *tiles)
-    start_plane(3, m_second)
-    start_rest(3, m_second)
-    sums_middle(1)
-    local_part(m_second, n)
-    finish(3, m_second, n)
+    start_rows(3, m_second)
+    local_part(m_second, n, lambda: sums_middle(1))
+    finish_rows(3, n)
     gamma_1, delta_1 = sums_end(1)
     beta_0 = gamma_1 / gamma_0
     alpha_1 = gamma_1 / (delta_1 - beta_0 * gamma_1 / alpha_0)
     step_1 = jnp.broadcast_to(alpha_1, (rows, width))
     ratio_1 = jnp.broadcast_to(beta_0, (rows, width))
 
-    def second_update(a, carry):
-        gamma, delta = carry
-        for b in range(4):
-            for c in range(4):
-                applied = w[a, b, c]
-                searched = applied + ratio_1 * s[a, b, c]
-                s[a, b, c] = searched
-                search = u[a, b, c] + ratio_1 * p[a, b, c]
-                p[a, b, c] = search
-                x[a, b, c] += step_1 * search
-                residual = r[a, b, c] - step_1 * searched
-                r[a, b, c] = residual
-                smooth = inv[a, b, c] * residual
-                u[a, b, c] = smooth
-                applied = applied - step_1 * (n[a, b, c] + ratio_1 * z[a, b, c])
-                w[a, b, c] = applied
-                gamma = gamma + residual * smooth
-                delta = delta + applied * smooth
-        return gamma, delta
-
-    tiles = carried_loop(second_update)
+    def second_update(a, b, c, powered):
+        applied = w[a, b, c]
+        searched = applied + ratio_1 * s[a, b, c]
+        s[a, b, c] = searched
+        search = u[a, b, c] + ratio_1 * p[a, b, c]
+        p[a, b, c] = search
+        x[a, b, c] += step_1 * search
+        residual = r[a, b, c] - step_1 * searched
+        r[a, b, c] = residual
+        smooth = inv[a, b, c] * residual
+        u[a, b, c] = smooth
+        applied = applied - step_1 * (powered + ratio_1 * z[a, b, c])
+        w[a, b, c] = applied
+        return applied, (residual * smooth, applied * smooth)
+
+    tiles = streamed(3, m_second, n, second_update, None, True)
     sums_begin(2, *tiles)
     sums_middle(2)
     lane_join = one_where(i1 == 4 * (i0 % part) + i0 // part)
@@ -492,7 +492,7 @@
                 [field[:, :, c, :, h * part:(h + 1) * part] for c in range(4)], axis=-1
             ).reshape(nodes, CHUNK)
             total = None
-            for piece in exact_pieces(wide):
+            for piece in exact_pieces(wide)[:2]:
                 moved = dot(piece, lane_join).astype(BF16)
                 moved = dot(row_join, moved)
                 total = moved if total is None else total + moved
@@ -537,12 +537,13 @@
                 pltpu.VMEM((ITERS, 8, 128), F32), pltpu.VMEM((ITERS, n_group - 1, 8, 128), F32),
                 pltpu.SemaphoreType.DMA((5,)),
                 pltpu.SemaphoreType.DMA((3,)), pltpu.SemaphoreType.DMA((3,)),
-                pltpu.SemaphoreType.DMA((APPLIES, 4)), pltpu.SemaphoreType.DMA((APPLIES, 4)),
+                pltpu.SemaphoreType.DMA((APPLIES, 4, 2)), pltpu.SemaphoreType.DMA((APPLIES, 4, 2)),
+                pltpu.SemaphoreType.DMA((APPLIES, 2)), pltpu.SemaphoreType.DMA((APPLIES, 2)),
                 pltpu.SemaphoreType.DMA((ITERS, n_rad - 1)), pltpu.SemaphoreType.DMA((ITERS, n_rad - 1)),
                 pltpu.SemaphoreType.DMA((ITERS, n_group - 1)), pltpu.SemaphoreType.DMA((ITERS, n_group - 1)),
             ],
             compiler_params=pltpu.CompilerParams(
-                collective_id=0, has_side_effects=True, vmem_limit_bytes=40 * 1024 * 1024
+                collective_id=0, has_side_effects=True, vmem_limit_bytes=63 * 1024 * 1024
             ),
             name="pcg",
         )(source_term, initial_guess, metric)

time: 55 us -> 53.1 us (0.965)
  local copies, waits for them, and re-layouts: 4.4 us -> 2.74 us
    unnamed x8 -> x4, local copies, waits for them, and re-layouts: 4.4 us -> 2.74 us
where the time goes in v2:
time: 53.1 us; the launch traced here: 53 us
  Pallas kernels  49.6 us (93%)
  local copies, waits for them, and re-layouts  2.74 us (5%)
  between operations  0.65 us (1%)
    pallas_call x1, Pallas kernels, local(): pl.pallas_call(functools.partial(kernel, n_group, n_rad), out_shape=[jax....  49.6 us
    unnamed x4, local copies, waits for them, and re-layouts  2.74 us

profile of v2, /device:TPU:0, one launch (start us, length us, event | category | flops | bytes accessed | tf_op | source)
XLA Modules:
  0.0 53.0 jit_solution(10393721883630730656)
XLA Ops:
  0.6 49.6 %pcg.1 = (f32[4,32,1024]{2,1,0:T(8,128)}, f32[4,32,1024]{2,1,0:T(8,128)}) custom-call(f32[4,32,1024]{2,1,0:T(8,128)} %source_hbm.1, f32[4,32,1024]{2,1,0:T(8,128)} %guess_hbm.1, f32[3,8,256]{2,1,0:T(8,128)} %bitcast.1), custom_call_target="tpu_custom_call" | custom-call | tf_op jit(solution)/shard_map/pcg/pallas_call | solution.py:525
  50.2 0.0 copy-start
  50.2 1.9 %copy.7 = f32[4,32,1024]{2,1,0:T(8,128)} copy(f32[4,32,1024]{2,1,0:T(8,128)} %get-tuple-element.4) | data formatting | bytes 1048576
  52.2 0.0 copy-done
  52.2 0.8 %copy.8 = f32[4,32,1024]{2,1,0:T(8,128)} copy(f32[4,32,1024]{2,1,0:T(8,128)S(1)} %copy-done) | data formatting | bytes 1048576
Async XLA Ops:
  50.2 2.0 %copy-start = (f32[4,32,1024]{2,1,0:T(8,128)S(1)}, f32[4,32,1024]{2,1,0:T(8,128)}, u32[]{:S(2)}) copy-start(f32[4,32,1024]{2,1,0:T(8,128)} %get-tuple-element.5) | copy-start | bytes 1572868
